TPU v7x, 32 devices: a whole 2x2x4 slice. The times are simulated.
32 devices in a mesh: expert: 4 (over x, core), shard: 8 (over z, y).
Axes of the slice: x: 2, y: 2, z: 4, core: 2. Of those that a mesh axis runs over, the one named last changes fastest.
Arguments:
- master_gate: float32 [64, 2048, 1024], P('expert', 'shard'), may hold values from -0.1875 to 0.1875
- master_up: float32 [64, 2048, 1024], P('expert', 'shard'), may hold values from -0.1875 to 0.1875
- master_down: float32 [64, 1024, 2048], P('expert', None, 'shard'), may hold values from -0.25 to 0.25
- router_weight: float32 [2048, 64], P('shard', 'expert'), may hold values from -0.125 to 0.125
- router_gain: float32 [2048], P('shard'), may hold values from 0.25 to 1.75
Outputs:
- final_gate: bfloat16 [64, 2048, 1024], P('expert', None, 'shard')
- final_up: bfloat16 [64, 2048, 1024], P('expert', None, 'shard')
- final_down: bfloat16 [64, 1024, 2048], P('expert', 'shard')
- scale_gate: float32 [64, 1024], P('expert', 'shard')
- scale_up: float32 [64, 1024], P('expert', 'shard')
- scale_down: float32 [64, 1024], P('expert', 'shard')
- serve_router: bfloat16 [2048, 64], replicated
All inputs are finite; a program needn't handle non-finite values.
Results may differ from a plain program's by a relative error of at most 0.001.
Values may be sent and summed in bfloat16 or wider, within the bound.
A program may use at most 192 MiB of HBM per device.

v0:
```python
import jax
import jax.numpy as jnp
from jax import lax
from jax.sharding import PartitionSpec as P


def on_device(master_gate, master_up, master_down, router_weight, router_gain):
    total_gate, total_up, total_down = lax.psum(
        (
            jnp.sum(master_gate * master_gate, axis=1),
            jnp.sum(master_up * master_up, axis=1),
            jnp.sum(master_down * master_down, axis=2),
        ),
        "shard",
    )
    scale_gate = jnp.sqrt(total_gate)
    scale_up = jnp.sqrt(total_up)
    scale_down = jnp.sqrt(total_down)
    narrow_gate, narrow_up, narrow_down = (
        (master_gate / jnp.expand_dims(scale_gate, 1)).astype(jnp.bfloat16),
        (master_up / jnp.expand_dims(scale_up, 1)).astype(jnp.bfloat16),
        (master_down / jnp.expand_dims(scale_down, 2)).astype(jnp.bfloat16),
    )
    final_gate, final_up = (
        lax.all_to_all(narrow_gate, "shard", split_axis=2, concat_axis=1, tiled=True),
        lax.all_to_all(narrow_up, "shard", split_axis=2, concat_axis=1, tiled=True),
    )
    final_down = lax.all_to_all(narrow_down, "shard", split_axis=1, concat_axis=2, tiled=True)
    scale_gate = lax.dynamic_slice_in_dim(
        scale_gate, lax.axis_index("shard") * final_gate.shape[2], final_gate.shape[2], axis=1
    )
    scale_up = lax.dynamic_slice_in_dim(
        scale_up, lax.axis_index("shard") * final_up.shape[2], final_up.shape[2], axis=1
    )
    scale_down = lax.dynamic_slice_in_dim(
        scale_down, lax.axis_index("shard") * final_down.shape[1], final_down.shape[1], axis=1
    )
    part_router = (router_weight * router_gain[:, None]).astype(jnp.bfloat16)
    row_router = lax.all_gather(part_router, "shard", axis=0, tiled=True)
    serve_router = lax.all_gather(row_router, "expert", axis=1, tiled=True)
    return (final_gate, final_up, final_down, scale_gate, scale_up, scale_down, serve_router)


def solution(mesh):
    placed = (
        P("expert", "shard", None),
        P("expert", "shard", None),
        P("expert", None, "shard"),
        P("shard", "expert"),
        P("shard"),
    )
    return jax.shard_map(
        on_device,
        mesh=mesh,
        in_specs=placed,
        out_specs=(
            P("expert", None, "shard"),
            P("expert", None, "shard"),
            P("expert", "shard", None),
            P("expert", "shard"),
            P("expert", "shard"),
            P("expert", "shard"),
            P(),
        ),
        check_vma=False,
    )
```

profile of v0, /device:TPU:0, one launch (start us, length us, event | category | flops | bytes accessed | tf_op | source)
XLA Modules:
  0.0 758.6 jit_solution(1279384502401970627)
XLA Ops:
  7.2 0.0 all-reduce.3.cloned.1.call-start
  7.2 8.6 %multiply_reduce_fusion = f32[16,1024]{1,0:T(8,128)} fusion(f32[16,1024,256]{2,1,0:T(8,128)} %param.7), kind=kLoop, calls=%fused_computation.2 | loop fusion | flops 8372224 | bytes 16842752 | tf_op jit(solution)/shard_map/reduce_sum | solution.py:12
  15.8 12.6 %multiply_reduce_fusion.1 = (f32[16,1024]{1,0:T(8,128)}, f32[16,1024]{1,0:T(8,128)}) fusion(f32[16,256,1024]{2,1,0:T(8,128)} %param.6, f32[16,256,1024]{2,1,0:T(8,128)} %param.5), kind=kLoop, calls=%fused_computation.4 | loop fusion | flops 16744448 | bytes 33685504 | tf_op jit(solution)/shard_map/reduce_sum | solution.py:11
  28.4 0.0 all-reduce.3.cloned.1.call-update
  28.4 17.6 %copy.19 = f32[16,256,1024]{1,0,2:T(8,128)} copy(f32[16,256,1024]{2,1,0:T(8,128)} %param.6) | data formatting | bytes 33554432 | tf_op args[1]
  46.0 56.7 %all-reduce.3.cloned.1.call-done = (f32[16,1024]{1,0:T(8,128)}, f32[16,1024]{1,0:T(8,128)}, f32[16,1024]{1,0:T(8,128)}) async-done(((f32[16,1024]{1,0:T(8,128)}, f32[16,1024]{1,0:T(8,128)}, f32[16,1024]{1,0:T(8,128)}), (f32[16,1024]{1,0:T(8,128)}, f32[16,1024]{1,0:T(8,128)}, f32[16,1024]{1,0:T(8,128)})) %all-reduce.3.cloned.1.call-update) | async-done | bytes 196624 | tf_op jit(solution)/shard_map/psum | solution.py:8
  102.7 0.9 sqrt.10
  103.6 0.2 copy.18
  103.8 9.6 %divide_convert_fusion = bf16[16,256,1024]{1,0,2:T(8,128)(2,1)} fusion(f32[16,256,1024]{1,0,2:T(8,128)} %copy.19, f32[16,1024]{0,1:T(8,128)S(1)} %copy.18), kind=kLoop, calls=%fused_computation.3 | loop fusion | flops 8388608 | bytes 25231360 | tf_op jit(solution)/shard_map/convert_element_type | solution.py:21
  113.4 4.9 all-to-all-start.1
  118.4 0.0 copy-start.1
  118.4 17.6 %copy.16 = f32[16,256,1024]{1,0,2:T(8,128)} copy(f32[16,256,1024]{2,1,0:T(8,128)} %param.5) | data formatting | bytes 33554432 | tf_op args[0]
  136.0 0.0 copy-done.1
  136.0 0.2 copy.15
  136.2 0.0 copy-start
  136.2 9.7 %divide_convert_fusion.1 = bf16[16,256,1024]{1,0,2:T(8,128)(2,1)} fusion(f32[16,256,1024]{1,0,2:T(8,128)} %copy.16, f32[16,1024]{0,1:T(8,128)S(1)} %copy.15), kind=kLoop, calls=%fused_computation.5 | loop fusion | flops 8388608 | bytes 25231360 | tf_op jit(solution)/shard_map/convert_element_type | solution.py:20
  145.9 153.8 %all-to-all-done.1 = bf16[16,256,1024]{1,0,2:T(8,128)(2,1)} async-done(((bf16[16,256,1024]{1,0,2:T(8,128)(2,1)}), bf16[16,256,1024]{1,0,2:T(8,128)(2,1)}, u32[]{:S(2)}, u32[]{:S(2)}) %all-to-all-start.1) | async-done | bytes 8388640 | tf_op jit(solution)/shard_map/all_to_all | solution.py:26
  299.7 4.9 all-to-all-start
  304.7 0.0 copy-done
  304.7 0.2 copy.21
  304.9 0.0 copy-start.2
  304.9 0.0 copy-start.3
  305.0 16.6 %fusion = bf16[16,1024,256]{2,0,1:T(8,128)(2,1)} fusion(f32[16,1024,256]{2,1,0:T(8,128)} %param.7, f32[16,1024]{0,1:T(8,128)S(1)} %copy.21), kind=kLoop, calls=%fused_computation.1 | loop fusion | flops 8388608 | bytes 25231360 | tf_op jit(solution)/shard_map/convert_element_type | solution.py:22
  321.6 165.1 %all-to-all-done = bf16[16,256,1024]{1,0,2:T(8,128)(2,1)} async-done(((bf16[16,256,1024]{1,0,2:T(8,128)(2,1)}), bf16[16,256,1024]{1,0,2:T(8,128)(2,1)}, u32[]{:S(2)}, u32[]{:S(2)}) %all-to-all-start) | async-done | bytes 8388640 | tf_op jit(solution)/shard_map/all_to_all | solution.py:25
  486.7 5.0 all-to-all-start.2
  491.7 0.0 copy-done.2
  491.8 0.0 copy-done.3
  491.8 202.1 %all_gather.6 = bf16[2048,16]{0,1:T(8,128)(2,1)S(1)} all-gather(bf16[256,16]{0,1:T(8,128)(2,1)S(1)} %multiply_convert_fusion), channel_id=1, replica_groups=mesh['expert'=4,'shard'=8] {'shard'}, dimensions={0}, use_global_device_ids=true | all-gather | bytes 73728 | tf_op jit(solution)/shard_map/all_gather | solution.py:39
  693.9 5.9 all_gather.7
  699.9 0.6 constant_dynamic-slice_fusion
  700.5 0.6 constant_dynamic-slice_fusion.1
  701.1 0.6 constant_dynamic-slice_fusion.2
  701.7 12.3 %copy.20 = bf16[16,8,256,128]{3,2,1,0:T(8,128)(2,1)} copy(bf16[16,8,256,128]{2,0,3,1:T(8,128)(2,1)} %bitcast.4) | data formatting | bytes 16777216 | tf_op jit(solution)/shard_map/all_to_all | solution.py:26
  713.9 12.3 %copy.17 = bf16[16,8,256,128]{3,2,1,0:T(8,128)(2,1)} copy(bf16[16,8,256,128]{2,0,3,1:T(8,128)(2,1)} %bitcast.1) | data formatting | bytes 16777216 | tf_op jit(solution)/shard_map/all_to_all | solution.py:25
  726.2 0.0 all-to-all-done.2
  726.2 11.4 %copy.23 = bf16[16,128,8,256]{3,2,1,0:T(8,128)(2,1)} copy(bf16[16,128,8,256]{3,0,1,2:T(8,128)(2,1)} %bitcast.7) | data formatting | bytes 16777216 | tf_op jit(solution)/shard_map/all_to_all | solution.py:28
  737.6 13.4 %all_to_all.50 = bf16[16,128,2048]{2,1,0:T(8,128)(2,1)} reshape(bf16[16,128,8,256]{3,2,1,0:T(8,128)(2,1)} %copy.23) | data formatting | bytes 16777216 | tf_op jit(solution)/shard_map/all_to_all | solution.py:28
  751.0 0.7 copy.31
  (3 shorter events, 0.0 us)
Async XLA Ops:
  7.2 95.5 %all-reduce.3.cloned.1.call-start = ((), (), s32[]{:S(2)}) async-start(), calls=%async_computation.3 | async-start | bytes 393216 | tf_op jit(solution)/shard_map/psum | solution.py:8
  113.4 186.3 %all-to-all-start.1 = ((bf16[16,256,1024]{1,0,2:T(8,128)(2,1)}), bf16[16,256,1024]{1,0,2:T(8,128)(2,1)}, u32[]{:S(2)}, u32[]{:S(2)}) async-start(bf16[16,256,1024]{1,0,2:T(8,128)(2,1)} %divide_convert_fusion), calls=%async_computation.1 | async-start | bytes 16777216 | tf_op jit(solution)/shard_map/all_to_all | solution.py:26
  118.4 17.6 %copy-start.1 = (f32[16,1024]{1,0:T(8,128)S(1)}, f32[16,1024]{1,0:T(8,128)}, u32[]{:S(2)}) copy-start(f32[16,1024]{1,0:T(8,128)} %get-tuple-element.7) | copy-start | bytes 196612
  136.2 168.5 %copy-start = (f32[16,1024]{1,0:T(8,128)S(1)}, f32[16,1024]{1,0:T(8,128)}, u32[]{:S(2)}) copy-start(f32[16,1024]{1,0:T(8,128)} %get-tuple-element.9) | copy-start | bytes 196612
  299.7 187.0 %all-to-all-start = ((bf16[16,256,1024]{1,0,2:T(8,128)(2,1)}), bf16[16,256,1024]{1,0,2:T(8,128)(2,1)}, u32[]{:S(2)}, u32[]{:S(2)}) async-start(bf16[16,256,1024]{1,0,2:T(8,128)(2,1)} %divide_convert_fusion.1), calls=%async_computation | async-start | bytes 16777216 | tf_op jit(solution)/shard_map/all_to_all | solution.py:25
  304.9 186.8 %copy-start.2 = (f32[256,16]{0,1:T(8,128)S(1)}, f32[256,16]{0,1:T(8,128)}, u32[]{:S(2)}) copy-start(f32[256,16]{0,1:T(8,128)} %param.8) | copy-start | bytes 49156
  304.9 186.8 %copy-start.3 = (f32[256]{0:T(256)S(1)}, f32[256]{0:T(256)}, u32[]{:S(2)}) copy-start(f32[256]{0:T(256)} %param.9) | copy-start | bytes 3076
  486.7 239.5 %all-to-all-start.2 = ((bf16[16,1024,256]{2,0,1:T(8,128)(2,1)}), bf16[16,1024,256]{2,0,1:T(8,128)(2,1)}, u32[]{:S(2)}, u32[]{:S(2)}) async-start(bf16[16,1024,256]{2,0,1:T(8,128)(2,1)} %fusion), calls=%async_computation.2 | async-start | bytes 16777216 | tf_op jit(solution)/shard_map/all_to_all | solution.py:28
Sparse Core Ops, SparseCore 0:
  28.6 74.0 all-reduce.2
where the time goes:
time: 760 us; the launch traced here: 759 us
  waiting for transfers between devices  376 us (49%)
  blocking collectives  208 us (27%)
  local copies, waits for them, and re-layouts  88.6 us (12%)
  other arithmetic  57.2 us (8%)
  starting transfers between devices  14.9 us (2%)
  between operations  14.2 us (2%)
    all_gather x1, blocking collectives, on_device(): row_router = lax.all_gather(part_router, 'shard', axis=0, tiled=True)  202 us
    all_to_all x1, waiting for transfers between devices, on_device(): lax.all_to_all(narrow_gate, 'shard', split_axis=2, concat_axis=1, tiled=T...  165 us
    all_to_all x1, waiting for transfers between devices, on_device(): lax.all_to_all(narrow_up, 'shard', split_axis=2, concat_axis=1, tiled=True)  154 us
    psum x1, waiting for transfers between devices, on_device(): lax.psum((jnp.sum(master_gate * master_gate, axis=1), jnp.sum(master_up *...  56.7 us
    unnamed x11, local copies, waits for them, and re-layouts  35.9 us
    all_to_all x2, local copies, waits for them, and re-layouts, on_device(): lax.all_to_all(narrow_down, 'shard', split_axis=1, concat_axis=2, tiled=T...  24.8 us
    convert_element_type x1, other arithmetic, on_device(): (master_down / jnp.expand_dims(scale_down, 2)).astype(jnp.bfloat16)  16.6 us
  transfers between devices with their start and end apart: 4, of which 3 were waited for; matrix products, arithmetic and copies ran while one was open for 12% of the time, Pallas kernels for 0%

commit v1 on v0

--- a/solution.py
+++ b/solution.py
@@ -23,7 +23,12 @@
     )
     final_gate, final_up = (
         lax.all_to_all(narrow_gate, "shard", split_axis=2, concat_axis=1, tiled=True),
-        lax.all_to_all(narrow_up, "shard", split_axis=2, concat_axis=1, tiled=True),
+        jnp.concatenate(
+            lax.all_to_all(
+                jnp.stack(jnp.split(narrow_up, lax.axis_size("shard"), axis=2)), "shard", 0, 0
+            ),
+            axis=1,
+        ),
     )
     final_down = lax.all_to_all(narrow_down, "shard", split_axis=1, concat_axis=2, tiled=True)
     scale_gate = lax.dynamic_slice_in_dim(

time: 760 us -> 756 us (level)
  local copies, waits for them, and re-layouts: 88.6 us -> 76.3 us
  waiting for transfers between devices: 376 us -> 386 us
    all_to_all x1 -> x0, local copies, waits for them, and re-layouts: 12.3 us -> none  [on_device(): lax.all_to_all(narrow_up, 'shard', split_axis=2, concat_axis=1, tiled=True)]
    all_to_all x1, waiting for transfers between devices: 154 us -> 165 us  [on_device(): lax.all_to_all(jnp.stack(jnp.split(narrow_up, lax.axis_size('shard'), axi...]
    unnamed x11 -> x17, local copies, waits for them, and re-layouts: 35.9 us -> 27 us
    reshape x0 -> x1, local copies, waits for them, and re-layouts: none -> 7.89 us  [on_device(): jnp.concatenate(lax.all_to_all(jnp.stack(jnp.split(narrow_up, lax.axis_si...]
  transfers between devices with their start and end apart: 4 -> 4, of which waited for: 3 -> 3; matrix products, arithmetic and copies ran while one was open for 12% -> 10% of each run, Pallas kernels for 0% -> 0%
where the time goes in v1:
time: 756 us; the launch traced here: 754 us
  waiting for transfers between devices  386 us (51%)
  blocking collectives  208 us (28%)
  local copies, waits for them, and re-layouts  76.3 us (10%)
  other arithmetic  54.7 us (7%)
  starting transfers between devices  15.2 us (2%)
  between operations  14.2 us (2%)
    all_gather x1, blocking collectives, on_device(): row_router = lax.all_gather(part_router, 'shard', axis=0, tiled=True)  202 us
    all_to_all x1, waiting for transfers between devices, on_device(): lax.all_to_all(jnp.stack(jnp.split(narrow_up, lax.axis_size('shard'), axi...  165 us
    all_to_all x1, waiting for transfers between devices, on_device(): lax.all_to_all(narrow_gate, 'shard', split_axis=2, concat_axis=1, tiled=T...  164 us
    psum x1, waiting for transfers between devices, on_device(): lax.psum((jnp.sum(master_gate * master_gate, axis=1), jnp.sum(master_up *...  56.7 us
    unnamed x17, local copies, waits for them, and re-layouts  27 us
    all_to_all x2, local copies, waits for them, and re-layouts, on_device(): lax.all_to_all(narrow_down, 'shard', split_axis=1, concat_axis=2, tiled=T...  24.8 us
    convert_element_type x1, other arithmetic, on_device(): (master_down / jnp.expand_dims(scale_down, 2)).astype(jnp.bfloat16)  16.6 us
  transfers between devices with their start and end apart: 4, of which 3 were waited for; matrix products, arithmetic and copies ran while one was open for 10% of the time, Pallas kernels for 0%

profile of v1, /device:TPU:0, one launch (start us, length us, event | category | flops | bytes accessed | tf_op | source)
XLA Modules:
  0.0 754.3 jit_solution(11293946100042297443)
XLA Ops:
  7.2 0.0 all-reduce.3.cloned.1.call-start
  7.2 8.6 %multiply_reduce_fusion = f32[16,1024]{1,0:T(8,128)} fusion(f32[16,1024,256]{2,1,0:T(8,128)} %param.7), kind=kLoop, calls=%fused_computation.2 | loop fusion | flops 8372224 | bytes 16842752 | tf_op jit(solution)/shard_map/reduce_sum | solution.py:12
  15.8 12.6 %multiply_reduce_fusion.1 = (f32[16,1024]{1,0:T(8,128)}, f32[16,1024]{1,0:T(8,128)}) fusion(f32[16,256,1024]{2,1,0:T(8,128)} %param.6, f32[16,256,1024]{2,1,0:T(8,128)} %param.5), kind=kLoop, calls=%fused_computation.4 | loop fusion | flops 16744448 | bytes 33685504 | tf_op jit(solution)/shard_map/reduce_sum | solution.py:11
  28.4 0.0 all-reduce.3.cloned.1.call-update
  28.4 17.6 %copy.16 = f32[16,256,1024]{1,0,2:T(8,128)} copy(f32[16,256,1024]{2,1,0:T(8,128)} %param.5) | data formatting | bytes 33554432 | tf_op args[0]
  46.0 56.7 %all-reduce.3.cloned.1.call-done = (f32[16,1024]{1,0:T(8,128)}, f32[16,1024]{1,0:T(8,128)}, f32[16,1024]{1,0:T(8,128)}) async-done(((f32[16,1024]{1,0:T(8,128)}, f32[16,1024]{1,0:T(8,128)}, f32[16,1024]{1,0:T(8,128)}), (f32[16,1024]{1,0:T(8,128)}, f32[16,1024]{1,0:T(8,128)}, f32[16,1024]{1,0:T(8,128)})) %all-reduce.3.cloned.1.call-update) | async-done | bytes 196624 | tf_op jit(solution)/shard_map/psum | solution.py:8
  102.7 0.9 sqrt.9
  103.6 0.2 copy.15
  103.8 9.6 %divide_convert_fusion.1 = bf16[16,256,1024]{1,0,2:T(8,128)(2,1)} fusion(f32[16,256,1024]{1,0,2:T(8,128)} %copy.16, f32[16,1024]{0,1:T(8,128)S(1)} %copy.15), kind=kLoop, calls=%fused_computation.5 | loop fusion | flops 8388608 | bytes 25231360 | tf_op jit(solution)/shard_map/convert_element_type | solution.py:20
  113.4 0.0 copy-start.1
  113.4 5.1 all-to-all-start
  118.5 0.0 copy-done.1
  118.5 7.2 divide_convert_fusion
  125.8 1.2 fusion.8
  127.0 1.2 fusion.7
  128.3 1.2 fusion.6
  129.5 1.2 fusion.5
  130.8 1.2 fusion.4
  132.0 1.2 fusion.3
  133.3 1.2 fusion.2
  134.5 1.2 fusion.1
  135.8 0.0 copy-start
  135.8 164.1 %all-to-all-done = bf16[16,256,1024]{1,0,2:T(8,128)(2,1)} async-done(((bf16[16,256,1024]{1,0,2:T(8,128)(2,1)}), bf16[16,256,1024]{1,0,2:T(8,128)(2,1)}, u32[]{:S(2)}, u32[]{:S(2)}) %all-to-all-start) | async-done | bytes 8388640 | tf_op jit(solution)/shard_map/all_to_all | solution.py:25
  299.9 5.0 all-to-all-start.1
  304.9 0.0 copy-done
  304.9 0.2 copy.19
  305.1 16.6 %fusion = bf16[16,1024,256]{2,0,1:T(8,128)(2,1)} fusion(f32[16,1024,256]{2,1,0:T(8,128)} %param.7, f32[16,1024]{0,1:T(8,128)S(1)} %copy.19), kind=kLoop, calls=%fused_computation.1 | loop fusion | flops 8388608 | bytes 25231360 | tf_op jit(solution)/shard_map/convert_element_type | solution.py:22
  321.8 0.0 copy-start.2
  321.8 0.0 copy-start.3
  321.8 165.1 %all-to-all-done.1 = bf16[8,16,256,128]{3,2,1,0:T(8,128)(2,1)} async-done(((bf16[8,16,256,128]{3,2,1,0:T(8,128)(2,1)}), bf16[8,16,256,128]{3,2,1,0:T(8,128)(2,1)}, u32[]{:S(2)}, u32[]{:S(2)}) %all-to-all-start.1) | async-done | bytes 8388640 | tf_op jit(solution)/shard_map/all_to_all | solution.py:27
  486.8 5.1 all-to-all-start.2
  492.0 0.0 copy-done.2
  492.0 0.0 copy-done.3
  492.0 202.2 %all_gather.6 = bf16[2048,16]{0,1:T(8,128)(2,1)S(1)} all-gather(bf16[256,16]{0,1:T(8,128)(2,1)S(1)} %multiply_convert_fusion), channel_id=1, replica_groups=mesh['expert'=4,'shard'=8] {'shard'}, dimensions={0}, use_global_device_ids=true | all-gather | bytes 73728 | tf_op jit(solution)/shard_map/all_gather | solution.py:44
  694.2 5.8 all_gather.7
  700.0 0.6 constant_dynamic-slice_fusion.2
  700.6 0.6 constant_dynamic-slice_fusion.1
  701.2 0.6 constant_dynamic-slice_fusion
  701.8 12.3 %copy.17 = bf16[16,8,256,128]{3,2,1,0:T(8,128)(2,1)} copy(bf16[16,8,256,128]{2,0,3,1:T(8,128)(2,1)} %bitcast.1) | data formatting | bytes 16777216 | tf_op jit(solution)/shard_map/all_to_all | solution.py:25
  714.1 7.9 %copy.18 = bf16[16,8,256,128]{3,2,1,0:T(8,128)(2,1)} copy(bf16[16,8,256,128]{3,2,0,1:T(8,128)(2,1)} %bitcast.11) | data formatting | bytes 16777216 | tf_op jit(solution)/shard_map/reshape | solution.py:26
  721.9 0.0 all-to-all-done.2
  722.0 11.4 %copy.21 = bf16[16,128,8,256]{3,2,1,0:T(8,128)(2,1)} copy(bf16[16,128,8,256]{3,0,1,2:T(8,128)(2,1)} %bitcast.14) | data formatting | bytes 16777216 | tf_op jit(solution)/shard_map/all_to_all | solution.py:33
  733.3 13.4 %all_to_all.37 = bf16[16,128,2048]{2,1,0:T(8,128)(2,1)} reshape(bf16[16,128,8,256]{3,2,1,0:T(8,128)(2,1)} %copy.21) | data formatting | bytes 16777216 | tf_op jit(solution)/shard_map/all_to_all | solution.py:33
  746.7 0.7 copy.36
  (3 shorter events, 0.1 us)
Async XLA Ops:
  7.2 95.5 %all-reduce.3.cloned.1.call-start = ((), (), s32[]{:S(2)}) async-start(), calls=%async_computation.3 | async-start | bytes 393216 | tf_op jit(solution)/shard_map/psum | solution.py:8
  113.4 5.1 copy-start.1
  113.4 186.5 %all-to-all-start = ((bf16[16,256,1024]{1,0,2:T(8,128)(2,1)}), bf16[16,256,1024]{1,0,2:T(8,128)(2,1)}, u32[]{:S(2)}, u32[]{:S(2)}) async-start(bf16[16,256,1024]{1,0,2:T(8,128)(2,1)} %divide_convert_fusion.1), calls=%async_computation | async-start | bytes 16777216 | tf_op jit(solution)/shard_map/all_to_all | solution.py:25
  135.8 169.1 %copy-start = (f32[16,1024]{1,0:T(8,128)S(1)}, f32[16,1024]{1,0:T(8,128)}, u32[]{:S(2)}) copy-start(f32[16,1024]{1,0:T(8,128)} %get-tuple-element.9) | copy-start | bytes 196612
  299.9 187.0 %all-to-all-start.1 = ((bf16[8,16,256,128]{3,2,1,0:T(8,128)(2,1)}), bf16[8,16,256,128]{3,2,1,0:T(8,128)(2,1)}, u32[]{:S(2)}, u32[]{:S(2)}) async-start(bf16[8,16,256,128]{3,2,1,0:T(8,128)(2,1)} %fusion.1), calls=%async_computation.1 | async-start | bytes 16777216 | tf_op jit(solution)/shard_map/all_to_all | solution.py:27
  321.8 170.2 %copy-start.2 = (f32[256,16]{0,1:T(8,128)S(1)}, f32[256,16]{0,1:T(8,128)}, u32[]{:S(2)}) copy-start(f32[256,16]{0,1:T(8,128)} %param.8) | copy-start | bytes 49156
  321.8 170.2 %copy-start.3 = (f32[256]{0:T(256)S(1)}, f32[256]{0:T(256)}, u32[]{:S(2)}) copy-start(f32[256]{0:T(256)} %param.9) | copy-start | bytes 3076
  486.8 235.1 %all-to-all-start.2 = ((bf16[16,1024,256]{2,0,1:T(8,128)(2,1)}), bf16[16,1024,256]{2,0,1:T(8,128)(2,1)}, u32[]{:S(2)}, u32[]{:S(2)}) async-start(bf16[16,1024,256]{2,0,1:T(8,128)(2,1)} %fusion), calls=%async_computation.2 | async-start | bytes 16777216 | tf_op jit(solution)/shard_map/all_to_all | solution.py:33
Sparse Core Ops, SparseCore 0:
  28.6 74.0 all-reduce.2
